TPU v7x, 32 devices: a whole 2x2x4 slice. The times are simulated.
32 devices in a mesh: gx: 8 (over y, x, core), gy: 4 (over z).
Axes of the slice: x: 2, y: 2, z: 4, core: 2. Of those that a mesh axis runs over, the one named last changes fastest.
Arguments:
- object_field: float32 [2, 256, 512], P(None, 'gy', 'gx'), may hold values from -1 to 1
- probe_modes: float32 [2, 1024, 128], P(None, ('gy', 'gx')), may hold values from -1.5 to 1.5
- positions: int32 [4, 8, 12, 2], P('gy', 'gx'), may hold values from 4 to 60, as said below
- amplitudes: float32 [4, 8, 12, 128, 128], P('gy', 'gx'), may hold values from 0 to 2
Outputs:
- object_out: float32 [2, 256, 512], P(None, 'gy', 'gx')
- probe_out: float32 [2, 1024, 128], P(None, ('gy', 'gx'))
Inputs may be any that keep to these rules, and one draw needn't show every extreme that they name: `positions`: each entry is a (row, column) inside its own tile; the centres of one tile lie at distinct cells of the 16 grid, each moved from the cell's middle by at most 4 cells along each dimension.
All inputs are finite; a program needn't handle non-finite values.
Results may differ from a plain program's by a relative error of at most 0.00065.
The roundings to bfloat16 on the way count: a program that leaves them out, or rounds other values in their place, can miss the bound.
Values sent between devices are 32-bit elements; how exact they have to be, the bound alone decides.
A program may use at most 64 MiB of HBM per device.

v0:
```python
import math

import jax
import jax.numpy as jnp
from jax import lax
from jax.experimental import pallas as pl
from jax.experimental.pallas import tpu as pltpu
from jax.sharding import PartitionSpec as P

MODES = 8
ITERS = 2
SUBLANES = 8


SOFT_FLOOR = 0.05
OBJECT_REG = 1.0
PROBE_REG = 1.0


def from_behind(block, axis, distance):
    devices = range(lax.axis_size(axis))
    route = [(i - distance, i) for i in devices if i - distance in devices]
    return lax.ppermute(block, axis, route)


def extended_2(array, sides, width):
    for axis, dim in sides:
        peers, length = (lax.axis_size(axis), array.shape[dim])
        up = [(i, (i + 1) % peers) for i in range(peers - 1)]
        down = [(j, i) for i, j in up]
        last = lax.slice_in_dim(array, length - width, length, axis=dim)
        initial = lax.slice_in_dim(array, 0, width, axis=dim)
        before = lax.ppermute(last, axis, up)
        after = lax.ppermute(initial, axis, down)
        array = jnp.concatenate([before, array, after], axis=dim)
    return array


def tables(probe_side, sign_flip):
    indices = jnp.arange(probe_side, dtype=jnp.int32)
    phases = indices[:, None] * indices[None, :] % probe_side
    angles = phases.astype(jnp.float32) * (2.0 * math.pi / probe_side)
    factor = 1.0 / math.sqrt(probe_side)
    cosine = jnp.cos(angles) * factor
    sine_part = sign_flip * jnp.sin(angles) * factor
    left_op = jnp.stack(
        [jnp.stack([cosine, -sine_part]), jnp.stack([sine_part, cosine])]
    ).transpose(0, 2, 1, 3)
    right_op = jnp.stack(
        [jnp.stack([cosine, sine_part]), jnp.stack([-sine_part, cosine])]
    ).transpose(0, 2, 1, 3)
    return (left_op.astype(jnp.bfloat16), right_op.astype(jnp.bfloat16))


def visit_kernel(places, ext_ref, probe_ref, measured_ref, fwd_left, fwd_right, inv_left, inv_right,
                 grad_obj_ref, grad_probe_ref, weight_probe_ref, far_ref, weight_obj_ref):
    count, side, _ = measured_ref.shape
    modes = probe_ref.shape[1] // side
    lanes = ext_ref.shape[2]
    grad_obj_ref[...] = jnp.zeros_like(grad_obj_ref)
    grad_probe_ref[...] = jnp.zeros_like(grad_probe_ref)
    weight_probe_ref[...] = jnp.zeros_like(weight_probe_ref)
    weight = jnp.zeros((side, side), jnp.float32)
    for m in range(modes):
        p_real = probe_ref[0, m * side : (m + 1) * side, :]
        p_imag = probe_ref[1, m * side : (m + 1) * side, :]
        weight += p_real * p_real + p_imag * p_imag
    weight_obj_ref[...] = weight

    def dot(left, right):
        return jnp.dot(left, right, preferred_element_type=jnp.float32)

    def two_sided(left_op, right_op, pair):
        half = dot(left_op[...], pair).astype(jnp.bfloat16)
        results = []
        for k in range(2):
            block = half[:, k * side : (k + 1) * side]
            rows = jnp.concatenate([block[:side], block[side:]], axis=1)
            results.append(dot(rows, right_op[...]))
        return results

    def visit(j, carry):
        row_at = places[j, 0]
        col_at = places[j, 1]
        tall = side + SUBLANES
        shift = lax.rem(row_at, SUBLANES)
        window = pl.ds(pl.multiple_of(row_at - shift, SUBLANES), tall)
        right = lax.rem(lanes - col_at, lanes)
        up = lax.rem(tall - shift, tall)

        def patch_of(i):
            columns = pltpu.roll(ext_ref[i, window, :], right, 1)[:, :side]
            return pltpu.roll(columns, up, 0)[:side]

        o_real = patch_of(0)
        o_imag = patch_of(1)
        weight_probe_ref[...] += o_real * o_real + o_imag * o_imag
        intensity = jnp.zeros((side, side), jnp.float32)
        for m in range(0, modes, 2):
            columns = []
            for k in (m, m + 1):
                p_real = probe_ref[0, k * side : (k + 1) * side, :]
                p_imag = probe_ref[1, k * side : (k + 1) * side, :]
                w_real = (p_real * o_real - p_imag * o_imag).astype(jnp.bfloat16)
                w_imag = (p_real * o_imag + p_imag * o_real).astype(jnp.bfloat16)
                columns.append(jnp.concatenate([w_real, w_imag], axis=0))
            for k, far in enumerate(two_sided(fwd_left, fwd_right, jnp.concatenate(columns, axis=1))):
                far_ref[(m + k) * side : (m + k + 1) * side, :] = far
                intensity += far[:, :side] * far[:, :side] + far[:, side:] * far[:, side:]
        shrink = 1.0 - measured_ref[j] / jnp.sqrt(intensity + SOFT_FLOOR)
        g_real = jnp.zeros((side, side), jnp.float32)
        g_imag = jnp.zeros((side, side), jnp.float32)
        for m in range(0, modes, 2):
            columns = []
            for k in (m, m + 1):
                rows = slice(k * side, (k + 1) * side)
                r_real = (far_ref[rows, :side] * shrink).astype(jnp.bfloat16)
                r_imag = (far_ref[rows, side:] * shrink).astype(jnp.bfloat16)
                columns.append(jnp.concatenate([r_real, r_imag], axis=0))
            for k, change in enumerate(two_sided(inv_left, inv_right, jnp.concatenate(columns, axis=1))):
                rows = slice((m + k) * side, (m + k + 1) * side)
                p_real = probe_ref[0, rows, :]
                p_imag = probe_ref[1, rows, :]
                c_real = change[:, :side]
                c_imag = change[:, side:]
                g_real += p_real * c_real + p_imag * c_imag
                g_imag += p_real * c_imag - p_imag * c_real
                grad_probe_ref[0, rows, :] += o_real * c_real + o_imag * c_imag
                grad_probe_ref[1, rows, :] += o_real * c_imag - o_imag * c_real
        short = jnp.zeros((SUBLANES, side), jnp.float32)
        blank = jnp.zeros((tall, lanes - side), jnp.float32)
        for i, part in enumerate((g_real, g_imag, weight_obj_ref[...])):
            part = jnp.concatenate([part, short], axis=0)
            wide = jnp.concatenate([pltpu.roll(part, shift, 0), blank], axis=1)
            grad_obj_ref[i, window, :] += pltpu.roll(wide, col_at, 1)
        return carry

    lax.fori_loop(0, count, visit, 0)


def flat(operators):
    left_op, right_op = operators
    side = left_op.shape[1]
    return (left_op.reshape(2 * side, 2 * side), right_op.reshape(2 * side, 2 * side))


def gradients(extended, probe, places, measured, forward, inverse):
    side = measured.shape[-1]
    vmem = pl.BlockSpec(memory_space=pltpu.VMEM)
    rows, lanes = extended.shape[1:]
    flops = measured.shape[0] * 4 * 2 * (2 * side) ** 2 * probe.shape[1]
    return pl.pallas_call(
        visit_kernel,
        out_shape=(
            jax.ShapeDtypeStruct((3, rows, lanes), jnp.float32),
            jax.ShapeDtypeStruct(probe.shape, jnp.float32),
            jax.ShapeDtypeStruct((side, side), jnp.float32),
        ),
        in_specs=[pl.BlockSpec(memory_space=pltpu.SMEM)] + [vmem] * 7,
        out_specs=(vmem, vmem, vmem),
        scratch_shapes=[
            pltpu.VMEM((probe.shape[1], 2 * side), jnp.float32),
            pltpu.VMEM((side, side), jnp.float32),
        ],
        compiler_params=pltpu.CompilerParams(vmem_limit_bytes=32 * 1024 * 1024),
        cost_estimate=pl.CostEstimate(flops=flops, bytes_accessed=4 * 1024 * 1024, transcendentals=0),
        name="visits",
    )(places, extended, probe, measured, *forward, *inverse)


def fold_rows(gradient, margin, tile_side):
    extent = gradient.shape[1]
    for direction in (1, -1):
        rim_part = gradient[:, extent - margin :, :] if direction == 1 else gradient[:, :margin, :]
        offset = margin if direction == 1 else tile_side
        arrived = from_behind(rim_part, "gy", direction)
        gradient = gradient.at[:, offset : offset + margin, :].add(arrived)
    return gradient[:, margin : margin + tile_side, :]


def fold_cols(gradient, margin, tile_side):
    extent = gradient.shape[2]
    for direction in (1, -1):
        rim_part = gradient[:, :, extent - margin :] if direction == 1 else gradient[:, :, :margin]
        offset = margin if direction == 1 else tile_side
        arrived = from_behind(rim_part, "gx", direction)
        gradient = gradient.at[:, :, offset : offset + margin].add(arrived)
    return gradient[:, :, margin : margin + tile_side]


def whole_of(own):
    planes, rows, side = own.shape
    blocks = own
    for axis in ("gy", "gx"):
        copies = jnp.broadcast_to(blocks[None], (lax.axis_size(axis), *blocks.shape))
        blocks = lax.all_to_all(copies, axis, 0, 0, tiled=True)
    return blocks.transpose(2, 1, 0, 3, 4).reshape(planes, -1, side)


def scattered_sum(terms):
    planes, rows, side = terms.shape
    down, across = lax.axis_size("gy"), lax.axis_size("gx")
    terms = terms.reshape(planes, down, across, rows // (down * across), side)
    terms = terms.transpose(2, 0, 1, 3, 4)
    terms = lax.all_to_all(terms, "gx", 0, 0, tiled=True).sum(axis=0)
    terms = terms.transpose(1, 0, 2, 3)
    return lax.all_to_all(terms, "gy", 0, 0, tiled=True).sum(axis=0)


def local(object_field, probe_modes, positions, amplitudes):
    probe_side = amplitudes.shape[-1]
    margin = probe_side // 2
    tile_side = object_field.shape[1]
    lanes = -(-(tile_side + probe_side) // 128) * 128
    places = positions.reshape(-1, 2)
    measured = amplitudes.reshape(-1, probe_side, probe_side)
    forward = flat(tables(probe_side, -1.0))
    inverse = flat(tables(probe_side, 1.0))
    own = probe_modes
    probe = whole_of(own)
    current = object_field
    for iteration in range(ITERS):
        extended = extended_2(current, (("gy", 1), ("gx", 2)), margin)
        extended = jnp.pad(extended, ((0, 0), (0, 0), (0, lanes - extended.shape[2])))
        grad_obj, grad_probe, weight_probe = gradients(
            extended, probe, places, measured, forward, inverse
        )
        grad_obj = grad_obj[:, :, : tile_side + probe_side]
        folded = fold_cols(fold_rows(grad_obj, margin, tile_side), margin, tile_side)
        current = current - folded[0:2] / (folded[2] + OBJECT_REG)
        weights = jnp.tile(weight_probe, (MODES, 1))[None]
        totals = scattered_sum(jnp.concatenate([grad_probe, weights]))
        own = own - totals[0:2] / (totals[2:3] + PROBE_REG)
        if iteration < ITERS - 1:
            probe = whole_of(own)
    return (current, own)


def solution(mesh):
    return jax.shard_map(
        local,
        mesh=mesh,
        in_specs=(
            P(None, "gy", "gx"),
            P(None, ("gy", "gx"), None),
            P("gy", "gx", None, None),
            P("gy", "gx", None, None, None),
        ),
        out_specs=(P(None, "gy", "gx"), P(None, ("gy", "gx"), None)),
        check_vma=False,
    )
```

profile of v0, /device:TPU:0, one launch (start us, length us, event | category | flops | bytes accessed | tf_op | source)
XLA Modules:
  0.0 194.0 jit_solution(10627423148108234133)
XLA Ops:
  1.9 5.6 %collective-permute-start = (f32[2,64,64]{2,1,0:T(8,128)}, f32[2,64,64]{2,1,0:T(8,128)S(1)}, u32[]{:S(2)}, u32[]{:S(2)}) collective-permute-start(f32[2,64,64]{2,1,0:T(8,128)} %param.20), channel_id=1, source_target_pairs={{0,1},{1,2},{2,3},{4,5},{5,6},{6,7},{8,9},{9,10},{10,11},{12,13},{... | collective-permute-start | bytes 98312 | tf_op jit(solution)/shard_map/ppermute | solution.py:33
  8.9 4.3 %all-to-all-start = ((f32[4,2,32,128]{3,2,1,0:T(8,128)}), f32[4,2,32,128]{3,2,1,0:T(8,128)S(1)}, u32[]{:S(2)}, u32[]{:S(2)}) async-start(f32[4,2,32,128]{3,2,1,0:T(8,128)} %broadcast_in_dim.8), calls=%async_computation | async-start | bytes 262144 | tf_op jit(solution)/shard_map/all_to_all | solution.py:196
  14.3 4.9 %all-to-all-done = f32[4,2,32,128]{3,2,1,0:T(8,128)S(1)} async-done(((f32[4,2,32,128]{3,2,1,0:T(8,128)}), f32[4,2,32,128]{3,2,1,0:T(8,128)S(1)}, u32[]{:S(2)}, u32[]{:S(2)}) %all-to-all-start) | async-done | bytes 131104 | tf_op jit(solution)/shard_map/all_to_all | solution.py:196
  20.3 3.9 %all-to-all-start.1 = ((f32[8,4,2,32,128]{4,3,1,2,0:T(8,128)}), f32[8,4,2,32,128]{4,3,1,2,0:T(8,128)S(1)}, u32[]{:S(2)}, u32[]{:S(2)}) async-start(f32[8,4,2,32,128]{4,3,1,2,0:T(8,128)} %broadcast_in_dim.9), calls=%async_computation.1 | async-start | bytes 2097152 | tf_op jit(solution)/shard_map/all_to_all | solution.py:196
  26.3 3.0 %collective-permute-start.2 = (f32[2,192,64]{2,1,0:T(8,128)S(1)}, f32[2,192,64]{2,1,0:T(8,128)S(1)}, u32[]{:S(2)}, u32[]{:S(2)}) collective-permute-start(f32[2,192,64]{2,1,0:T(8,128)S(1)} %constant_dynamic-update-slice_fusion), channel_id=1, source_target_pairs={{0,4},{4,8},{8,12},{12,16},{16,20},{20,24},{24,28},{1,5},{5,9},{9,... | collective-permute-start | bytes 294920 | tf_op jit(solution)/shard_map/ppermute | solution.py:33
  30.6 8.9 %all-to-all-done.1 = f32[8,4,2,32,128]{4,3,1,2,0:T(8,128)S(1)} async-done(((f32[8,4,2,32,128]{4,3,1,2,0:T(8,128)}), f32[8,4,2,32,128]{4,3,1,2,0:T(8,128)S(1)}, u32[]{:S(2)}, u32[]{:S(2)}) %all-to-all-start.1) | async-done | bytes 1048608 | tf_op jit(solution)/shard_map/all_to_all | solution.py:196
  39.6 20.0 %visits.2 = (f32[3,192,256]{2,1,0:T(8,128)S(1)}, f32[2,1024,128]{2,1,0:T(8,128)S(1)}, f32[128,128]{1,0:T(8,128)S(1)}) custom-call(s32[12,2]{1,0:T(8,128)S(1)} %copy.44.places, f32[2,192,256]{2,1,0:T(8,128)S(1)} %select_maximum_fusion.4.ext_ref, f32[2,1024,128]{2,1,0:T(8,128)S(1)} %bitcast.71, f32[12,128,128]{2,1,0:T(8,128)S(1)} %bitcast.80, ...), custom_call_target="tpu_custom_call" | custom-call | flops 6442450944 | bytes 4194304 | tf_op jit(solution)/shard_map/visits/pallas_call | solution.py:152
  61.0 5.7 %all-to-all-start.2 = ((f32[8,3,4,32,128]{4,3,2,1,0:T(8,128)}), f32[8,3,4,32,128]{4,3,2,1,0:T(8,128)S(1)}, u32[]{:S(2)}, u32[]{:S(2)}) async-start(f32[8,3,4,32,128]{4,3,2,1,0:T(8,128)} %copy_bitcast_fusion.1), calls=%async_computation.2 | async-start | bytes 3145728 | tf_op jit(solution)/shard_map/all_to_all | solution.py:205
  67.5 3.9 %collective-permute-start.4 = (f32[3,64,192]{2,1,0:T(8,128)}, f32[3,64,192]{2,1,0:T(8,128)}, u32[]{:S(2)}, u32[]{:S(2)}) collective-permute-start(f32[3,64,192]{2,1,0:T(8,128)} %get-tuple-element.112), channel_id=1, source_target_pairs={{0,1},{1,2},{2,3},{4,5},{5,6},{6,7},{8,9},{9,10},{10,11},{12,13},{... | collective-permute-start | bytes 442376 | tf_op jit(solution)/shard_map/ppermute | solution.py:23
  72.6 15.1 %all-to-all-done.2 = f32[8,3,4,32,128]{4,3,2,1,0:T(8,128)S(1)} async-done(((f32[8,3,4,32,128]{4,3,2,1,0:T(8,128)}), f32[8,3,4,32,128]{4,3,2,1,0:T(8,128)S(1)}, u32[]{:S(2)}, u32[]{:S(2)}) %all-to-all-start.2) | async-done | bytes 1572896 | tf_op jit(solution)/shard_map/all_to_all | solution.py:205
  90.2 3.4 %all-to-all-start.3 = ((f32[4,3,32,128]{3,2,1,0:T(8,128)}), f32[4,3,32,128]{3,2,1,0:T(8,128)S(1)}, u32[]{:S(2)}, u32[]{:S(2)}) async-start(f32[4,3,32,128]{3,2,1,0:T(8,128)} %copy.47), calls=%async_computation.3 | async-start | bytes 393216 | tf_op jit(solution)/shard_map/all_to_all | solution.py:207
  94.6 5.1 %all-to-all-done.3 = f32[4,3,32,128]{3,2,1,0:T(8,128)S(1)} async-done(((f32[4,3,32,128]{3,2,1,0:T(8,128)}), f32[4,3,32,128]{3,2,1,0:T(8,128)S(1)}, u32[]{:S(2)}, u32[]{:S(2)}) %all-to-all-start.3) | async-done | bytes 196640 | tf_op jit(solution)/shard_map/all_to_all | solution.py:207
  100.5 3.3 %all-to-all-start.4 = ((f32[4,2,32,128]{3,2,1,0:T(8,128)}), f32[4,2,32,128]{3,2,1,0:T(8,128)S(1)}, u32[]{:S(2)}, u32[]{:S(2)}) async-start(f32[4,2,32,128]{3,2,1,0:T(8,128)} %broadcast_in_dim.10), calls=%async_computation.4 | async-start | bytes 262144 | tf_op jit(solution)/shard_map/all_to_all | solution.py:196
  106.4 3.3 %all-to-all-done.4 = f32[4,2,32,128]{3,2,1,0:T(8,128)S(1)} async-done(((f32[4,2,32,128]{3,2,1,0:T(8,128)}), f32[4,2,32,128]{3,2,1,0:T(8,128)S(1)}, u32[]{:S(2)}, u32[]{:S(2)}) %all-to-all-start.4) | async-done | bytes 131104 | tf_op jit(solution)/shard_map/all_to_all | solution.py:196
  110.8 3.6 %all-to-all-start.5 = ((f32[8,4,2,32,128]{4,3,1,2,0:T(8,128)}), f32[8,4,2,32,128]{4,3,1,2,0:T(8,128)S(1)}, u32[]{:S(2)}, u32[]{:S(2)}) async-start(f32[8,4,2,32,128]{4,3,1,2,0:T(8,128)} %broadcast_in_dim.11), calls=%async_computation.5 | async-start | bytes 2097152 | tf_op jit(solution)/shard_map/all_to_all | solution.py:196
  115.8 4.5 %collective-permute-start.8 = (f32[2,64,64]{2,1,0:T(8,128)S(1)}, f32[2,64,64]{2,1,0:T(8,128)S(1)}, u32[]{:S(2)}, u32[]{:S(2)}) collective-permute-start(f32[2,64,64]{2,1,0:T(8,128)S(1)} %fusion.14), channel_id=1, source_target_pairs={{0,1},{1,2},{2,3},{4,5},{5,6},{6,7},{8,9},{9,10},{10,11},{12,13},{... | collective-permute-start | bytes 98312 | tf_op jit(solution)/shard_map/ppermute | solution.py:33
  129.8 20.0 %visits.3 = (f32[3,192,256]{2,1,0:T(8,128)S(1)}, f32[2,1024,128]{2,1,0:T(8,128)S(1)}, f32[128,128]{1,0:T(8,128)S(1)}) custom-call(s32[12,2]{1,0:T(8,128)S(1)} %copy.44.places, f32[2,192,256]{2,1,0:T(8,128)S(1)} %select_maximum_fusion.ext_ref, f32[2,1024,128]{2,1,0:T(8,128)S(1)} %bitcast.70, f32[12,128,128]{2,1,0:T(8,128)S(1)} %bitcast.81, ...), custom_call_target="tpu_custom_call" | custom-call | flops 6442450944 | bytes 4194304 | tf_op jit(solution)/shard_map/visits/pallas_call | solution.py:152
  151.3 6.3 %all-to-all-start.6 = ((f32[8,3,4,32,128]{4,3,2,1,0:T(8,128)}), f32[8,3,4,32,128]{4,3,2,1,0:T(8,128)S(1)}, u32[]{:S(2)}, u32[]{:S(2)}) async-start(f32[8,3,4,32,128]{4,3,2,1,0:T(8,128)} %copy_bitcast_fusion), calls=%async_computation.6 | async-start | bytes 3145728 | tf_op jit(solution)/shard_map/all_to_all | solution.py:205
  157.6 3.9 %collective-permute-start.12 = (f32[3,64,192]{2,1,0:T(8,128)S(1)}, f32[3,64,192]{2,1,0:T(8,128)S(1)}, u32[]{:S(2)}, u32[]{:S(2)}) collective-permute-start(f32[3,64,192]{2,1,0:T(8,128)S(1)} %get-tuple-element.110), channel_id=1, source_target_pairs={{0,1},{1,2},{2,3},{4,5},{5,6},{6,7},{8,9},{9,10},{10,11},{12,13},{... | collective-permute-start | bytes 442376 | tf_op jit(solution)/shard_map/ppermute | solution.py:23
  162.7 3.5 %collective-permute-done.12 = f32[3,64,192]{2,1,0:T(8,128)S(1)} collective-permute-done((f32[3,64,192]{2,1,0:T(8,128)S(1)}, f32[3,64,192]{2,1,0:T(8,128)S(1)}, u32[]{:S(2)}, u32[]{:S(2)}) %collective-permute-start.12) | collective-permute-done | bytes 147488 | tf_op jit(solution)/shard_map/ppermute | solution.py:23
  166.2 4.1 %collective-permute-done.13 = f32[3,64,192]{2,1,0:T(8,128)S(1)} collective-permute-done((f32[3,64,192]{2,1,0:T(8,128)S(1)}, f32[3,64,192]{2,1,0:T(8,128)S(1)}, u32[]{:S(2)}, u32[]{:S(2)}) %collective-permute-start.13) | collective-permute-done | bytes 147488 | tf_op jit(solution)/shard_map/ppermute | solution.py:23
  173.0 3.7 %collective-permute-done.15 = f32[3,64,64]{2,1,0:T(8,128)S(1)} collective-permute-done((f32[3,64,64]{2,1,0:T(8,128)S(1)}, f32[3,64,64]{2,1,0:T(8,128)S(1)}, u32[]{:S(2)}, u32[]{:S(2)}) %collective-permute-start.15) | collective-permute-done | bytes 49184 | tf_op jit(solution)/shard_map/ppermute | solution.py:23
  179.4 5.3 %all-to-all-start.7 = ((f32[4,3,32,128]{3,2,1,0:T(8,128)}), f32[4,3,32,128]{3,2,1,0:T(8,128)S(1)}, u32[]{:S(2)}, u32[]{:S(2)}) async-start(f32[4,3,32,128]{3,2,1,0:T(8,128)} %copy.53), calls=%async_computation.7 | async-start | bytes 393216 | tf_op jit(solution)/shard_map/all_to_all | solution.py:207
  185.3 8.1 %all-to-all-done.7 = f32[4,3,32,128]{3,2,1,0:T(8,128)S(1)} async-done(((f32[4,3,32,128]{3,2,1,0:T(8,128)}), f32[4,3,32,128]{3,2,1,0:T(8,128)S(1)}, u32[]{:S(2)}, u32[]{:S(2)}) %all-to-all-start.7) | async-done | bytes 196640 | tf_op jit(solution)/shard_map/all_to_all | solution.py:207
  (91 shorter events, 39.6 us)
Async XLA Ops:
  0.6 24.4 %collective-permute-start.1 = (f32[2,64,64]{2,1,0:T(8,128)}, f32[2,64,64]{2,1,0:T(8,128)S(1)}, u32[]{:S(2)}, u32[]{:S(2)}) collective-permute-start(f32[2,64,64]{2,1,0:T(8,128)} %param.20), channel_id=1, source_target_pairs={{1,0},{2,1},{3,2},{5,4},{6,5},{7,6},{9,8},{10,9},{11,10},{13,12},{... | collective-permute-start | bytes 98312 | tf_op jit(solution)/shard_map/ppermute | solution.py:34
  1.9 23.0 %collective-permute-start = (f32[2,64,64]{2,1,0:T(8,128)}, f32[2,64,64]{2,1,0:T(8,128)S(1)}, u32[]{:S(2)}, u32[]{:S(2)}) collective-permute-start(f32[2,64,64]{2,1,0:T(8,128)} %param.20), channel_id=1, source_target_pairs={{0,1},{1,2},{2,3},{4,5},{5,6},{6,7},{8,9},{9,10},{10,11},{12,13},{... | collective-permute-start | bytes 98312 | tf_op jit(solution)/shard_map/ppermute | solution.py:33
  8.9 10.2 %all-to-all-start = ((f32[4,2,32,128]{3,2,1,0:T(8,128)}), f32[4,2,32,128]{3,2,1,0:T(8,128)S(1)}, u32[]{:S(2)}, u32[]{:S(2)}) async-start(f32[4,2,32,128]{3,2,1,0:T(8,128)} %broadcast_in_dim.8), calls=%async_computation | async-start | bytes 262144 | tf_op jit(solution)/shard_map/all_to_all | solution.py:196
  20.3 19.2 %all-to-all-start.1 = ((f32[8,4,2,32,128]{4,3,1,2,0:T(8,128)}), f32[8,4,2,32,128]{4,3,1,2,0:T(8,128)S(1)}, u32[]{:S(2)}, u32[]{:S(2)}) async-start(f32[8,4,2,32,128]{4,3,1,2,0:T(8,128)} %broadcast_in_dim.9), calls=%async_computation.1 | async-start | bytes 2097152 | tf_op jit(solution)/shard_map/all_to_all | solution.py:196
  25.0 4.7 %collective-permute-start.3 = (f32[2,192,64]{2,1,0:T(8,128)S(1)}, f32[2,192,64]{2,1,0:T(8,128)S(1)}, u32[]{:S(2)}, u32[]{:S(2)}) collective-permute-start(f32[2,192,64]{2,1,0:T(8,128)S(1)} %constant_dynamic-update-slice_fusion), channel_id=1, source_target_pairs={{4,0},{8,4},{12,8},{16,12},{20,16},{24,20},{28,24},{5,1},{9,5},{13... | collective-permute-start | bytes 294920 | tf_op jit(solution)/shard_map/ppermute | solution.py:34
  26.3 4.1 %collective-permute-start.2 = (f32[2,192,64]{2,1,0:T(8,128)S(1)}, f32[2,192,64]{2,1,0:T(8,128)S(1)}, u32[]{:S(2)}, u32[]{:S(2)}) collective-permute-start(f32[2,192,64]{2,1,0:T(8,128)S(1)} %constant_dynamic-update-slice_fusion), channel_id=1, source_target_pairs={{0,4},{4,8},{8,12},{12,16},{16,20},{20,24},{24,28},{1,5},{5,9},{9,... | collective-permute-start | bytes 294920 | tf_op jit(solution)/shard_map/ppermute | solution.py:33
  61.0 26.7 %all-to-all-start.2 = ((f32[8,3,4,32,128]{4,3,2,1,0:T(8,128)}), f32[8,3,4,32,128]{4,3,2,1,0:T(8,128)S(1)}, u32[]{:S(2)}, u32[]{:S(2)}) async-start(f32[8,3,4,32,128]{4,3,2,1,0:T(8,128)} %copy_bitcast_fusion.1), calls=%async_computation.2 | async-start | bytes 3145728 | tf_op jit(solution)/shard_map/all_to_all | solution.py:205
  67.5 26.0 %collective-permute-start.4 = (f32[3,64,192]{2,1,0:T(8,128)}, f32[3,64,192]{2,1,0:T(8,128)}, u32[]{:S(2)}, u32[]{:S(2)}) collective-permute-start(f32[3,64,192]{2,1,0:T(8,128)} %get-tuple-element.112), channel_id=1, source_target_pairs={{0,1},{1,2},{2,3},{4,5},{5,6},{6,7},{8,9},{9,10},{10,11},{12,13},{... | collective-permute-start | bytes 442376 | tf_op jit(solution)/shard_map/ppermute | solution.py:23
  71.4 22.2 %collective-permute-start.5 = (f32[3,64,192]{2,1,0:T(8,128)}, f32[3,64,192]{2,1,0:T(8,128)}, u32[]{:S(2)}, u32[]{:S(2)}) collective-permute-start(f32[3,64,192]{2,1,0:T(8,128)} %get-tuple-element.113), channel_id=1, source_target_pairs={{1,0},{2,1},{3,2},{5,4},{6,5},{7,6},{9,8},{10,9},{11,10},{13,12},{... | collective-permute-start | bytes 442376 | tf_op jit(solution)/shard_map/ppermute | solution.py:23
  90.2 9.6 %all-to-all-start.3 = ((f32[4,3,32,128]{3,2,1,0:T(8,128)}), f32[4,3,32,128]{3,2,1,0:T(8,128)S(1)}, u32[]{:S(2)}, u32[]{:S(2)}) async-start(f32[4,3,32,128]{3,2,1,0:T(8,128)} %copy.47), calls=%async_computation.3 | async-start | bytes 393216 | tf_op jit(solution)/shard_map/all_to_all | solution.py:207
  100.5 9.2 %all-to-all-start.4 = ((f32[4,2,32,128]{3,2,1,0:T(8,128)}), f32[4,2,32,128]{3,2,1,0:T(8,128)S(1)}, u32[]{:S(2)}, u32[]{:S(2)}) async-start(f32[4,2,32,128]{3,2,1,0:T(8,128)} %broadcast_in_dim.10), calls=%async_computation.4 | async-start | bytes 262144 | tf_op jit(solution)/shard_map/all_to_all | solution.py:196
  103.8 10.6 %collective-permute-start.6 = (f32[3,64,64]{2,1,0:T(8,128)S(1)}, f32[3,64,64]{2,1,0:T(8,128)S(1)}, u32[]{:S(2)}, u32[]{:S(2)}) collective-permute-start(f32[3,64,64]{2,1,0:T(8,128)S(1)} %get-tuple-element.116), channel_id=1, source_target_pairs={{0,4},{4,8},{8,12},{12,16},{16,20},{20,24},{24,28},{1,5},{5,9},{9,... | collective-permute-start | bytes 147464 | tf_op jit(solution)/shard_map/ppermute | solution.py:23
  105.1 9.3 %collective-permute-start.7 = (f32[3,64,64]{2,1,0:T(8,128)S(1)}, f32[3,64,64]{2,1,0:T(8,128)S(1)}, u32[]{:S(2)}, u32[]{:S(2)}) collective-permute-start(f32[3,64,64]{2,1,0:T(8,128)S(1)} %get-tuple-element.117), channel_id=1, source_target_pairs={{4,0},{8,4},{12,8},{16,12},{20,16},{24,20},{28,24},{5,1},{9,5},{13... | collective-permute-start | bytes 147464 | tf_op jit(solution)/shard_map/ppermute | solution.py:23
  110.8 19.0 %all-to-all-start.5 = ((f32[8,4,2,32,128]{4,3,1,2,0:T(8,128)}), f32[8,4,2,32,128]{4,3,1,2,0:T(8,128)S(1)}, u32[]{:S(2)}, u32[]{:S(2)}) async-start(f32[8,4,2,32,128]{4,3,1,2,0:T(8,128)} %broadcast_in_dim.11), calls=%async_computation.5 | async-start | bytes 2097152 | tf_op jit(solution)/shard_map/all_to_all | solution.py:196
  114.5 6.4 %collective-permute-start.9 = (f32[2,64,64]{2,1,0:T(8,128)S(1)}, f32[2,64,64]{2,1,0:T(8,128)S(1)}, u32[]{:S(2)}, u32[]{:S(2)}) collective-permute-start(f32[2,64,64]{2,1,0:T(8,128)S(1)} %fusion.14), channel_id=1, source_target_pairs={{1,0},{2,1},{3,2},{5,4},{6,5},{7,6},{9,8},{10,9},{11,10},{13,12},{... | collective-permute-start | bytes 98312 | tf_op jit(solution)/shard_map/ppermute | solution.py:34
  115.8 6.4 %collective-permute-start.8 = (f32[2,64,64]{2,1,0:T(8,128)S(1)}, f32[2,64,64]{2,1,0:T(8,128)S(1)}, u32[]{:S(2)}, u32[]{:S(2)}) collective-permute-start(f32[2,64,64]{2,1,0:T(8,128)S(1)} %fusion.14), channel_id=1, source_target_pairs={{0,1},{1,2},{2,3},{4,5},{5,6},{6,7},{8,9},{9,10},{10,11},{12,13},{... | collective-permute-start | bytes 98312 | tf_op jit(solution)/shard_map/ppermute | solution.py:33
  122.3 4.4 %collective-permute-start.11 = (f32[2,192,64]{2,1,0:T(8,128)S(1)}, f32[2,192,64]{2,1,0:T(8,128)S(1)}, u32[]{:S(2)}, u32[]{:S(2)}) collective-permute-start(f32[2,192,64]{2,1,0:T(8,128)S(1)} %pad_maximum_fusion.2), channel_id=1, source_target_pairs={{4,0},{8,4},{12,8},{16,12},{20,16},{24,20},{28,24},{5,1},{9,5},{13... | collective-permute-start | bytes 294920 | tf_op jit(solution)/shard_map/ppermute | solution.py:34
  123.6 4.1 %collective-permute-start.10 = (f32[2,192,64]{2,1,0:T(8,128)S(1)}, f32[2,192,64]{2,1,0:T(8,128)S(1)}, u32[]{:S(2)}, u32[]{:S(2)}) collective-permute-start(f32[2,192,64]{2,1,0:T(8,128)S(1)} %pad_maximum_fusion.2), channel_id=1, source_target_pairs={{0,4},{4,8},{8,12},{12,16},{16,20},{20,24},{24,28},{1,5},{5,9},{9,... | collective-permute-start | bytes 294920 | tf_op jit(solution)/shard_map/ppermute | solution.py:33
  151.3 27.3 %all-to-all-start.6 = ((f32[8,3,4,32,128]{4,3,2,1,0:T(8,128)}), f32[8,3,4,32,128]{4,3,2,1,0:T(8,128)S(1)}, u32[]{:S(2)}, u32[]{:S(2)}) async-start(f32[8,3,4,32,128]{4,3,2,1,0:T(8,128)} %copy_bitcast_fusion), calls=%async_computation.6 | async-start | bytes 3145728 | tf_op jit(solution)/shard_map/all_to_all | solution.py:205
  157.6 8.7 %collective-permute-start.12 = (f32[3,64,192]{2,1,0:T(8,128)S(1)}, f32[3,64,192]{2,1,0:T(8,128)S(1)}, u32[]{:S(2)}, u32[]{:S(2)}) collective-permute-start(f32[3,64,192]{2,1,0:T(8,128)S(1)} %get-tuple-element.110), channel_id=1, source_target_pairs={{0,1},{1,2},{2,3},{4,5},{5,6},{6,7},{8,9},{9,10},{10,11},{12,13},{... | collective-permute-start | bytes 442376 | tf_op jit(solution)/shard_map/ppermute | solution.py:23
  161.4 8.9 %collective-permute-start.13 = (f32[3,64,192]{2,1,0:T(8,128)S(1)}, f32[3,64,192]{2,1,0:T(8,128)S(1)}, u32[]{:S(2)}, u32[]{:S(2)}) collective-permute-start(f32[3,64,192]{2,1,0:T(8,128)S(1)} %get-tuple-element.111), channel_id=1, source_target_pairs={{1,0},{2,1},{3,2},{5,4},{6,5},{7,6},{9,8},{10,9},{11,10},{13,12},{... | collective-permute-start | bytes 442376 | tf_op jit(solution)/shard_map/ppermute | solution.py:23
  170.4 2.6 %collective-permute-start.14 = (f32[3,64,64]{2,1,0:T(8,128)S(1)}, f32[3,64,64]{2,1,0:T(8,128)S(1)}, u32[]{:S(2)}, u32[]{:S(2)}) collective-permute-start(f32[3,64,64]{2,1,0:T(8,128)S(1)} %get-tuple-element.114), channel_id=1, source_target_pairs={{0,4},{4,8},{8,12},{12,16},{16,20},{20,24},{24,28},{1,5},{5,9},{9,... | collective-permute-start | bytes 147464 | tf_op jit(solution)/shard_map/ppermute | solution.py:23
  171.7 5.1 %collective-permute-start.15 = (f32[3,64,64]{2,1,0:T(8,128)S(1)}, f32[3,64,64]{2,1,0:T(8,128)S(1)}, u32[]{:S(2)}, u32[]{:S(2)}) collective-permute-start(f32[3,64,64]{2,1,0:T(8,128)S(1)} %get-tuple-element.115), channel_id=1, source_target_pairs={{4,0},{8,4},{12,8},{16,12},{20,16},{24,20},{28,24},{5,1},{9,5},{13... | collective-permute-start | bytes 147464 | tf_op jit(solution)/shard_map/ppermute | solution.py:23
  179.4 14.0 %all-to-all-start.7 = ((f32[4,3,32,128]{3,2,1,0:T(8,128)}), f32[4,3,32,128]{3,2,1,0:T(8,128)S(1)}, u32[]{:S(2)}, u32[]{:S(2)}) async-start(f32[4,3,32,128]{3,2,1,0:T(8,128)} %copy.53), calls=%async_computation.7 | async-start | bytes 393216 | tf_op jit(solution)/shard_map/all_to_all | solution.py:207
  (4 other events, 26.2 us)
where the time goes:
time: 195 us; the launch traced here: 194 us
  starting transfers between devices  72.5 us (37%)
  waiting for transfers between devices  63.8 us (33%)
  Pallas kernels  40 us (21%)
  local copies, waits for them, and re-layouts  8.44 us (4%)
  other arithmetic  8.1 us (4%)
    pallas_call x2, Pallas kernels, gradients(): pl.pallas_call(visit_kernel, out_shape=(jax.ShapeDtypeStruct((3, rows, la...  40 us
    all_to_all x4, waiting for transfers between devices, whole_of(): blocks = lax.all_to_all(copies, axis, 0, 0, tiled=True)  18.9 us
    all_to_all x2, waiting for transfers between devices, scattered_sum(): terms = lax.all_to_all(terms, 'gx', 0, 0, tiled=True).sum(axis=0)  16.7 us
    ppermute x4, starting transfers between devices, extended_2(): before = lax.ppermute(last, axis, up)  16.2 us
    ppermute x8, starting transfers between devices, from_behind(): return lax.ppermute(block, axis, route)  15.5 us
    all_to_all x4, starting transfers between devices, whole_of(): blocks = lax.all_to_all(copies, axis, 0, 0, tiled=True)  15.1 us
    all_to_all x2, waiting for transfers between devices, scattered_sum(): return lax.all_to_all(terms, 'gy', 0, 0, tiled=True).sum(axis=0)  13.2 us
    all_to_all x2, starting transfers between devices, scattered_sum(): terms = lax.all_to_all(terms, 'gx', 0, 0, tiled=True).sum(axis=0)  12 us
  transfers between devices with their start and end apart: 24, of which 15 were waited for; matrix products, arithmetic and copies ran while one was open for 6% of the time, Pallas kernels for 0%

commit v1 on v0

v1 whole, which is shorter than its diff:
```python
import functools
import math
from types import SimpleNamespace

import jax
import jax.numpy as jnp
import numpy as np
from jax import lax
from jax.experimental import pallas as pl
from jax.experimental.pallas import tpu as pltpu
from jax.sharding import PartitionSpec as P

ITERS = 2
SOFT_FLOOR = 0.05
OBJECT_REG = 1.0
PROBE_REG = 1.0
CHUNK = 16
MESH = pl.DeviceIdType.MESH
F32 = jnp.float32
BF16 = jnp.bfloat16


class Plan:
    def __init__(self, mesh, object_field, probe_modes, positions, amplitudes):
        self.gx, self.gy = mesh.shape["gx"], mesh.shape["gy"]
        self.side = amplitudes.shape[-1]
        self.count = amplitudes.shape[-3]
        self.tile = object_field.shape[1] // self.gy
        self.rows = probe_modes.shape[1]
        self.modes = self.rows // self.side
        self.own = self.rows // (self.gx * self.gy)
        self.chips = self.gx // 2
        self.split = self.own >= 8
        self.cores = 2 if self.split else 1
        self.piece = self.own if self.split else 2 * self.own
        self.block = self.rows // self.gy
        self.steps = min(self.modes, self.gy)
        self.step_modes = self.modes // self.steps
        self.step_blocks = self.gy // self.steps
        self.weights = max(1, self.side // self.block)
        self.weight_rows = self.weights * self.block
        self.quads = self.count // 4
        self.step_bodies = self.step_modes * self.quads
        assert self.tile * 2 == self.side and self.count % 4 == 0
        assert self.piece % 8 == 0 and self.gx % 2 == 0

    def scratch(self):
        s, n = self.side, self.count
        sems = pltpu.SemaphoreType.DMA
        k, c, g = self.piece, self.chips, self.gy
        vmem = pltpu.VMEM
        return dict(
            amp=vmem((n, s, s), F32),
            fwd=vmem((2 * s, 2 * s), BF16),
            inv=vmem((2 * s, 2 * s), BF16),
            probe=vmem((ITERS, 2, self.rows, s), F32),
            patch=vmem((n, 2, s, s), F32),
            ext=vmem((4, 3 * self.tile, s), F32),
            far=vmem((self.modes, n, s, 2 * s), F32),
            shrink=vmem((n, s, s), F32),
            delta=vmem((self.modes, n, s, 2 * s), F32),
            ops0=vmem((2 * s, 4 * s), BF16),
            ops1=vmem((2 * s, 4 * s), BF16),
            ops2=vmem((2 * s, 4 * s), BF16),
            mids0=vmem((4 * s, 2 * s), BF16),
            mids1=vmem((4 * s, 2 * s), BF16),
            mids2=vmem((4 * s, 2 * s), BF16),
            spread=vmem((n, 2, 2 * s, s), F32),
            weight=vmem((2 * s, s), F32),
            grad=vmem((ITERS, 2, self.rows, s), F32),
            wgrad=vmem((ITERS, 1, self.weight_rows, s), F32),
            obj=vmem((ITERS, self.tile, s), F32),
            halo=vmem((ITERS, 8, self.tile, s), F32),
            fold_tx=vmem((ITERS, 3, 3 * self.tile, s), F32),
            fold_rx=vmem((ITERS, 8, self.tile, s), F32),
            wfold_tx=vmem((ITERS, 3, 3 * self.tile, s), F32),
            wfold_rx=vmem((ITERS, 8, self.tile, s), F32),
            rx_a=vmem((ITERS, g, c, 2, k, s), F32),
            sum_a=vmem((ITERS, g, c, 2, k, s), F32),
            rx_b=vmem((ITERS, g, c - 1, 2, k, s), F32),
            sum_b=vmem((ITERS, g, 2, k, s), F32),
            rx_c=vmem((ITERS, g - 1, 2, k, s), F32),
            wrx_a=vmem((ITERS, self.weights, c, 1, k, s), F32),
            wsum_a=vmem((ITERS, self.weights, c, 1, k, s), F32),
            wrx_b=vmem((ITERS, self.weights, c - 1, 1, k, s), F32),
            wsum_b=vmem((ITERS, self.weights, 1, k, s), F32),
            wrx_c=vmem((ITERS, self.weights, g - 1, 1, k, s), F32),
            wsum=vmem((ITERS, self.weights, k, s), F32),
            load_sem=sems((3,)),
            a_sem=sems((2, ITERS, g)),
            b_sem=sems((2, ITERS, g)),
            c_sem=sems((2, ITERS, g)),
            wa_sem=sems((2, ITERS, self.weights)),
            wb_sem=sems((2, ITERS, self.weights)),
            wc_sem=sems((2, ITERS, self.weights)),
            row_sem=sems((ITERS, 1 + g)),
            gb_sem=sems((2, ITERS, g)),
            ga_sem=sems((2, ITERS, g)),
            halo_sem=sems((2, ITERS, 8)),
            fold_sem=sems((2, ITERS, 8)),
            wfold_sem=sems((2, ITERS, 8)),
        )


def aligned(value):
    return pl.multiple_of(value, 8)


def program(plan, names, places, object_ref, own_ref, amp_hbm, fwd_hbm, inv_hbm, object_out, probe_out, *scratch):
    r = SimpleNamespace(**dict(zip(names, scratch)))
    side, tile, piece, chips = plan.side, plan.tile, plan.piece, plan.chips
    nx, ny = plan.gx, plan.gy
    gx, gy = lax.axis_index("gx"), lax.axis_index("gy")
    chip, core = lax.div(gx, 2), lax.rem(gx, 2)
    lane = lax.broadcasted_iota(jnp.int32, (1, side), 1)
    low = lane < tile

    def half_turn(value):
        return pltpu.roll(value, tile, 1)

    def device(x, y):
        return {"gx": x, "gy": y}

    mate = device(gx + 1 - 2 * core, gy)
    chip_peers = [device(lax.rem(chip + d, chips) * 2 + core, gy) for d in range(1, chips)]
    row_peers = [device(gx, lax.rem(gy + d, ny)) for d in range(1, ny)]
    offsets = [(dy, dx) for dy in (-1, 0, 1) for dx in (-1, 0, 1) if (dy, dx) != (0, 0)]

    def inside(dy, dx):
        ok = gx >= 0
        if dy < 0:
            ok &= gy > 0
        if dy > 0:
            ok &= gy < ny - 1
        if dx < 0:
            ok &= gx > 0
        if dx > 0:
            ok &= gx < nx - 1
        return ok

    def send(source, target, sems, who):
        pltpu.make_async_remote_copy(
            src_ref=source, dst_ref=target, send_sem=sems[0], recv_sem=sems[1], device_id=who, device_id_type=MESH
        ).start()

    def await_bytes(ref, sem):
        pltpu.make_async_copy(ref, ref, sem).wait()

    loads = [
        pltpu.make_async_copy(amp_hbm, r.amp, r.load_sem.at[0]),
        pltpu.make_async_copy(fwd_hbm, r.fwd, r.load_sem.at[1]),
        pltpu.make_async_copy(inv_hbm, r.inv, r.load_sem.at[2]),
    ]
    for copy in loads:
        copy.start()

    for ref in (r.halo, r.fold_rx, r.wfold_rx):
        ref[...] = jnp.zeros(ref.shape, F32)

    def signal(who):
        pl.semaphore_signal(pltpu.get_barrier_semaphore(), inc=1, device_id=who, device_id_type=MESH)

    r.obj[0] = jnp.concatenate([object_ref[0], object_ref[1]], axis=1)
    home = lax.mul(lax.mul(gy, chips) + chip, plan.cores * piece) + (core * piece if plan.split else 0)
    for plane in range(2):
        r.probe[0, plane, pl.ds(aligned(home), piece), :] = own_ref[plane]

    greetings = 1 + (chips - 1) + (ny - 1)
    for who in [mate] + chip_peers + row_peers:
        signal(who)
    expected = greetings
    for dy, dx in offsets:
        ok = inside(dy, dx)
        expected = expected + ok.astype(jnp.int32)

        @pl.when(ok)
        def _():
            signal(device(gx + dx, gy + dy))

    r.grad[...] = jnp.zeros(r.grad.shape, F32)
    rim = jnp.zeros((tile, side), F32)
    r.weight[:tile] = rim
    r.weight[tile + side :] = rim

    def rims(j, carry):
        for plane in range(2):
            r.spread[j, plane, :tile] = rim
            r.spread[j, plane, tile + side :] = rim
        return carry

    lax.fori_loop(0, plan.count, rims, 0)
    pl.semaphore_wait(pltpu.get_barrier_semaphore(), expected)

    def to_neighbours(it, sources, target, sems):
        for n, (dy, dx) in enumerate(offsets):

            @pl.when(inside(dy, dx))
            def _():
                send(sources(dy, dx), target.at[it, n], (sems.at[0, it, n], sems.at[1, it, n]), device(gx + dx, gy + dy))

    def from_neighbours(it, target, sems):
        for n, (dy, dx) in enumerate(offsets):

            @pl.when(inside(-dy, -dx))
            def _():
                await_bytes(target.at[it, n], sems.at[1, it, n])

    def sent_to_neighbours(it, target, sems):
        for n, (dy, dx) in enumerate(offsets):

            @pl.when(inside(dy, dx))
            def _():
                await_bytes(target.at[it, n], sems.at[0, it, n])

    def rows_of(block, at_chip, at_core):
        start = (block * chips + at_chip) * (plan.cores * piece)
        return pl.ds(aligned(start + at_core * piece), piece)

    def my_core():
        return core if plan.split else 0

    def probe_piece(it, block):
        return r.probe.at[it, :, rows_of(block, chip, my_core())]

    def probe_span(it, pieces):
        return r.probe.at[it, :, pl.ds(0, pieces * piece)]

    def spread_chips(it, block):
        for who in chip_peers:
            send(probe_piece(it, block), probe_piece(it, block), (r.gb_sem.at[0, it, block], r.gb_sem.at[1, it, block]), who)

    def got_chips(it, block):
        await_bytes(probe_span(it, chips - 1), r.gb_sem.at[1, it, block])

    def spread_cores(it, block):
        if plan.split:
            for q in range(chips):
                view = r.probe.at[it, :, rows_of(block, q, core)]
                send(view, view, (r.ga_sem.at[0, it, block], r.ga_sem.at[1, it, block]), mate)

    def got_cores(it, block):
        if plan.split:
            await_bytes(probe_span(it, chips), r.ga_sem.at[1, it, block])

    def first_order(t):
        value, bit = 0, 1
        group = lax.div(gy, plan.step_blocks)
        while bit < plan.steps:
            value = value + bit * lax.rem(lax.div(group, bit) + lax.div(t, bit), 2)
            bit *= 2
        return value

    def blocks_of(step):
        return [step * plan.step_blocks + i for i in range(plan.step_blocks)]

    grads = SimpleNamespace(
        terms=r.grad,
        rx_a=r.rx_a,
        sum_a=r.sum_a,
        rx_b=r.rx_b,
        sum_b=r.sum_b,
        rx_c=r.rx_c,
        a_sem=r.a_sem,
        b_sem=r.b_sem,
        c_sem=r.c_sem,
    )
    weights = SimpleNamespace(
        terms=r.wgrad,
        rx_a=r.wrx_a,
        sum_a=r.wsum_a,
        rx_b=r.wrx_b,
        sum_b=r.wsum_b,
        rx_c=r.wrx_c,
        a_sem=r.wa_sem,
        b_sem=r.wb_sem,
        c_sem=r.wc_sem,
    )

    def reduce_a(ch, it, b):
        for q in range(chips):
            at_core = (1 - core) if plan.split else 0
            send(
                ch.terms.at[it, :, rows_of(b, q, at_core)],
                ch.rx_a.at[it, b, q],
                (ch.a_sem.at[0, it, b], ch.a_sem.at[1, it, b]),
                mate,
            )

    def reduce_b(ch, it, b):
        await_bytes(ch.rx_a.at[it, b], ch.a_sem.at[1, it, b])
        for q in range(chips):
            ch.sum_a[it, b, q] = ch.terms[it, :, rows_of(b, q, my_core()), :] + ch.rx_a[it, b, q]
        for d, who in enumerate(chip_peers):
            send(
                ch.sum_a.at[it, b, lax.rem(chip + d + 1, chips)],
                ch.rx_b.at[it, b, d],
                (ch.b_sem.at[0, it, b], ch.b_sem.at[1, it, b]),
                who,
            )

    def reduced_b(ch, it, b):
        await_bytes(ch.rx_b.at[it, b], ch.b_sem.at[1, it, b])
        total = ch.sum_a[it, b, chip]
        for d in range(chips - 1):
            total = total + ch.rx_b[it, b, d]
        ch.sum_b[it, b] = total

    def reduce_weights(it, w):
        reduced_b(weights, it, w)
        for d, who in enumerate(row_peers):
            send(
                weights.sum_b.at[it, w],
                weights.rx_c.at[it, w, d],
                (weights.c_sem.at[0, it, w], weights.c_sem.at[1, it, w]),
                who,
            )

    def settle_weights(it):
        for w in range(plan.weights):
            await_bytes(weights.rx_c.at[it, w], weights.c_sem.at[1, it, w])
            total = weights.sum_b[it, w]
            for d in range(ny - 1):
                total = total + weights.rx_c[it, w, d]
            r.wsum[it, w] = total[0] + PROBE_REG

    def to_owner(it, b):
        reduced_b(grads, it, b)

        @pl.when(gy != b)
        def _():
            slot = lax.rem(gy - b - 1 + ny, ny)
            send(
                grads.sum_b.at[it, b],
                grads.rx_c.at[it, slot],
                (grads.c_sem.at[0, it, b], grads.c_sem.at[1, it, 0]),
                device(gx, b),
            )

    def owned(it, b):
        await_bytes(grads.rx_c.at[it], grads.c_sem.at[1, it, 0])
        change = grads.sum_b[it, b]
        for d in range(ny - 1):
            change = change + grads.rx_c[it, d]
        place = rows_of(b, chip, my_core())
        down = r.wsum[it, lax.rem(b, plan.weights)]
        return [r.probe[it, plane, place, :] - change[plane] / down for plane in range(2)]

    def spread_rows(it, b):
        for who in row_peers:
            send(probe_piece(it, b), probe_piece(it, b), (r.row_sem.at[it, ny], r.row_sem.at[it, b]), who)

    def renew(b):
        @pl.when(gy == b)
        def _():
            new = owned(0, b)
            for plane in range(2):
                r.probe[1, plane, rows_of(b, chip, my_core()), :] = new[plane]
            spread_rows(1, b)
            spread_chips(1, b)

    def pass_chips(it, b):
        @pl.when(gy != b)
        def _():
            await_bytes(probe_piece(it, b), r.row_sem.at[it, b])
            spread_chips(it, b)

    def pass_cores(it, b):
        got_chips(it, b)
        spread_cores(it, b)

    grads = SimpleNamespace(
        terms=r.grad,
        rx_a=r.rx_a,
        sum_a=r.sum_a,
        rx_b=r.rx_b,
        sum_b=r.sum_b,
        rx_c=r.rx_c,
        a_sem=r.a_sem,
        b_sem=r.b_sem,
        c_sem=r.c_sem,
    )
    weights = SimpleNamespace(
        terms=r.wgrad,
        rx_a=r.wrx_a,
        sum_a=r.wsum_a,
        rx_b=r.wrx_b,
        sum_b=r.wsum_b,
        rx_c=r.wrx_c,
        a_sem=r.wa_sem,
        b_sem=r.wb_sem,
        c_sem=r.wc_sem,
    )

    def reduce_a(ch, it, b):
        for q in range(chips):
            at_core = (1 - core) if plan.split else 0
            send(
                ch.terms.at[it, :, rows_of(b, q, at_core)],
                ch.rx_a.at[it, b, q],
                (ch.a_sem.at[0, it, b], ch.a_sem.at[1, it, b]),
                mate,
            )

    def reduce_b(ch, it, b):
        await_bytes(ch.rx_a.at[it, b], ch.a_sem.at[1, it, b])
        for q in range(chips):
            ch.sum_a[it, b, q] = ch.terms[it, :, rows_of(b, q, my_core()), :] + ch.rx_a[it, b, q]
        for d, who in enumerate(chip_peers):
            send(
                ch.sum_a.at[it, b, lax.rem(chip + d + 1, chips)],
                ch.rx_b.at[it, b, d],
                (ch.b_sem.at[0, it, b], ch.b_sem.at[1, it, b]),
                who,
            )

    def reduced_b(ch, it, b):
        await_bytes(ch.rx_b.at[it, b], ch.b_sem.at[1, it, b])
        total = ch.sum_a[it, b, chip]
        for d in range(chips - 1):
            total = total + ch.rx_b[it, b, d]
        ch.sum_b[it, b] = total

    def reduce_weights(it, w):
        reduced_b(weights, it, w)
        for d, who in enumerate(row_peers):
            send(
                weights.sum_b.at[it, w],
                weights.rx_c.at[it, w, d],
                (weights.c_sem.at[0, it, w], weights.c_sem.at[1, it, w]),
                who,
            )

    def settle_weights(it):
        for w in range(plan.weights):
            await_bytes(weights.rx_c.at[it, w], weights.c_sem.at[1, it, w])
            total = weights.sum_b[it, w]
            for d in range(ny - 1):
                total = total + weights.rx_c[it, w, d]
            r.wsum[it, w] = total[0] + PROBE_REG

    def to_owner(it, b):
        reduced_b(grads, it, b)

        @pl.when(gy != b)
        def _():
            slot = lax.rem(gy - b - 1 + ny, ny)
            send(
                grads.sum_b.at[it, b],
                grads.rx_c.at[it, slot],
                (grads.c_sem.at[0, it, b], grads.c_sem.at[1, it, 0]),
                device(gx, b),
            )

    def owned(it, b):
        await_bytes(grads.rx_c.at[it], grads.c_sem.at[1, it, 0])
        change = grads.sum_b[it, b]
        for d in range(ny - 1):
            change = change + grads.rx_c[it, d]
        place = rows_of(b, chip, my_core())
        down = r.wsum[it, lax.rem(b, plan.weights)]
        return [r.probe[it, plane, place, :] - change[plane] / down for plane in range(2)]

    def spread_rows(it, b):
        for who in row_peers:
            send(probe_piece(it, b), probe_piece(it, b), (r.row_sem.at[it, ny], r.row_sem.at[it, b]), who)

    def renew(b):
        @pl.when(gy == b)
        def _():
            new = owned(0, b)
            for plane in range(2):
                r.probe[1, plane, rows_of(b, chip, my_core()), :] = new[plane]
            spread_rows(1, b)
            spread_chips(1, b)

    def pass_chips(it, b):
        @pl.when(gy != b)
        def _():
            await_bytes(probe_piece(it, b), r.row_sem.at[it, b])
            spread_chips(it, b)

    def pass_cores(it, b):
        got_chips(it, b)
        spread_cores(it, b)

    def over(step, act, *rest):
        if 0 <= step < plan.steps:
            for b in blocks_of(step):
                act(*rest, b)

    def widen(it):
        halo = {o: (lambda n: lambda: r.halo[it, n])(n) for n, o in enumerate(offsets)}
        for dy in (-1, 0, 1):
            left = halo[(-dy, 1)]()
            right = halo[(-dy, -1)]()
            centre = r.obj[it] if dy == 0 else halo[(-dy, 0)]()
            band = slice((dy + 1) * tile, (dy + 2) * tile)
            r.ext[0, band] = jnp.where(low, left, half_turn(centre))
            r.ext[1, band] = right
            r.ext[2, band] = jnp.where(low, half_turn(left), centre)
            r.ext[3, band] = half_turn(right)

    def cut_patches(it):
        def one(j, total):
            window = pl.ds(places[j, 0], side)
            col = places[j, 1]
            turn = lax.rem(side - col, side)
            for plane in range(2):
                one_half = pltpu.roll(r.ext[2 * plane, window, :], turn, 1)
                other = pltpu.roll(r.ext[2 * plane + 1, window, :], turn, 1)
                part = jnp.where(lane < side - col, one_half, other)
                r.patch[j, plane] = part
                total = total + part * part
            r.shrink[j] = jnp.zeros((side, side), F32)
            return total

        def some(i, total):
            for n in range(2):
                total = one(2 * i + n, total)
            return total

        total = lax.fori_loop(0, plan.count // 2, some, jnp.zeros((side, side), F32))
        for w in range(plan.weight_rows // side):
            r.wgrad[it, 0, w * side : (w + 1) * side, :] = total

    def sow(load, planes):
        lefts = [0.0] * planes
        rights = [0.0] * planes
        for j in range(plan.count):
            col = places[j, 1]
            for plane in range(planes):
                turned = pltpu.roll(load(j, plane), col, 1)
                lefts[plane] = lefts[plane] + jnp.where(lane >= col, turned, 0.0)
                rights[plane] = rights[plane] + jnp.where(lane < col, turned, 0.0)
        return (
            jnp.where(low, lefts[0], half_turn(lefts[-1])),
            jnp.where(low, half_turn(lefts[0]), lefts[-1]),
            jnp.where(low, rights[0], half_turn(rights[-1])),
        )

    band = tile

    def gather_rows(i, source):
        def load(j, plane):
            return source(j, plane, pl.ds(tile + i * band - places[j, 0], band))

        return load

    def fold_weights(it):
        total = jnp.zeros((side, side), F32)
        for m in range(plan.modes):
            for plane in range(2):
                part = r.probe[it, plane, m * side : (m + 1) * side, :]
                total = total + part * part
        r.weight[tile : tile + side] = total

        def rows_at(i, carry):
            tiles = sow(gather_rows(i, lambda j, plane, at: r.weight[at, :]), 1)
            for n in range(3):
                r.wfold_tx[it, n, pl.ds(aligned(i * band), band), :] = tiles[n]
            return carry

        lax.fori_loop(0, 3 * tile // band, rows_at, 0)
        to_neighbours(it, lambda dy, dx: r.wfold_tx.at[it, dx + 1, pl.ds((dy + 1) * tile, tile)], r.wfold_rx, r.wfold_sem)

    def fold_object(it):
        def rows_at(i, carry):
            tiles = sow(gather_rows(i, lambda j, plane, at: r.spread[j, plane, at, :]), 2)
            for n in range(3):
                r.fold_tx[it, n, pl.ds(aligned(i * band), band), :] = tiles[n]
            return carry

        lax.fori_loop(0, 3 * tile // band, rows_at, 0)
        to_neighbours(it, lambda dy, dx: r.fold_tx.at[it, dx + 1, pl.ds((dy + 1) * tile, tile)], r.fold_rx, r.fold_sem)

    def new_object(it):
        from_neighbours(it, r.wfold_rx, r.wfold_sem)
        from_neighbours(it, r.fold_rx, r.fold_sem)
        change = r.fold_tx[it, 1, tile : 2 * tile]
        down = r.wfold_tx[it, 1, tile : 2 * tile] + OBJECT_REG
        for n in range(8):
            change = change + r.fold_rx[it, n]
            down = down + r.wfold_rx[it, n]
        return r.obj[it] - change / down

    def send_object(it):
        to_neighbours(it, lambda dy, dx: r.obj.at[it], r.halo, r.halo_sem)

    def dot(left, right):
        return jnp.dot(left, right, preferred_element_type=F32)

    def quad(k, order):
        step = lax.div(k, plan.step_bodies)
        within = lax.rem(k, plan.step_bodies)
        return order(step) * plan.step_modes + lax.div(within, plan.quads), 4 * lax.rem(within, plan.quads)

    def half_way(operator, ops, mids):
        for h in range(2):
            half = dot(operator[...], ops[:, h * 2 * side : (h + 1) * 2 * side])
            for s in range(2):
                cols = slice(s * side, (s + 1) * side)
                target = slice((2 * h + s) * side, (2 * h + s + 1) * side)
                mids[target, :side] = half[:side, cols].astype(BF16)
                mids[target, side:] = half[side:, cols].astype(BF16)

    def chunk_rows(m, q):
        return pl.ds(pl.multiple_of(m * side + q * CHUNK, CHUNK), CHUNK)

    def waves(it, k, order, ops):
        m, j = quad(k, order)
        for q in range(side // CHUNK):
            upper = slice(q * CHUNK, (q + 1) * CHUNK)
            lower = slice(side + q * CHUNK, side + (q + 1) * CHUNK)
            p_re = r.probe[it, 0, chunk_rows(m, q), :]
            p_im = r.probe[it, 1, chunk_rows(m, q), :]
            for s in range(4):
                o_re = r.patch[j + s, 0, upper]
                o_im = r.patch[j + s, 1, upper]
                cols = slice(s * side, (s + 1) * side)
                ops[upper, cols] = (p_re * o_re - p_im * o_im).astype(BF16)
                ops[lower, cols] = (p_re * o_im + p_im * o_re).astype(BF16)

    def spectra(k, order, mids):
        m, j = quad(k, order)
        all_far = dot(mids[...], r.inv[...])
        for s in range(4):
            far = all_far[s * side : (s + 1) * side]
            r.far[m, j + s] = far
            r.shrink[j + s] += far[:, :side] * far[:, :side] + far[:, side:] * far[:, side:]

    def residuals(k, order, ops):
        m, j = quad(k, order)
        for q in range(side // CHUNK):
            upper = slice(q * CHUNK, (q + 1) * CHUNK)
            lower = slice(side + q * CHUNK, side + (q + 1) * CHUNK)
            for s in range(4):
                cols = slice(s * side, (s + 1) * side)
                scale = r.shrink[j + s, upper]
                far = r.far[m, j + s, upper, :]
                ops[upper, cols] = (far[:, :side] * scale).astype(BF16)
                ops[lower, cols] = (far[:, side:] * scale).astype(BF16)

    def changes(it, k, order, mids):
        m, j = quad(k, order)
        delta = dot(mids[...], r.fwd[...])
        for q in range(side // CHUNK):
            g_re = r.grad[it, 0, chunk_rows(m, q), :]
            g_im = r.grad[it, 1, chunk_rows(m, q), :]
            for s in range(4):
                upper = slice(q * CHUNK, (q + 1) * CHUNK)
                change = delta[s * side + q * CHUNK : s * side + (q + 1) * CHUNK]
                r.delta[m, j + s, upper, :] = change
                c_re, c_im = change[:, :side], change[:, side:]
                o_re = r.patch[j + s, 0, upper]
                o_im = r.patch[j + s, 1, upper]
                g_re = g_re + (o_re * c_re + o_im * c_im)
                g_im = g_im + (o_re * c_im - o_im * c_re)
            r.grad[it, 0, chunk_rows(m, q), :] = g_re
            r.grad[it, 1, chunk_rows(m, q), :] = g_im

    def object_terms(it, start, stop):
        def one(j, carry):
            for q in range(side // CHUNK):
                g_re = jnp.zeros((CHUNK, side), F32)
                g_im = jnp.zeros((CHUNK, side), F32)
                for m in range(plan.modes):
                    rows_q = slice(m * side + q * CHUNK, m * side + (q + 1) * CHUNK)
                    p_re = r.probe[it, 0, rows_q, :]
                    p_im = r.probe[it, 1, rows_q, :]
                    change = r.delta[m, j, q * CHUNK : (q + 1) * CHUNK, :]
                    c_re, c_im = change[:, :side], change[:, side:]
                    g_re = g_re + (p_re * c_re + p_im * c_im)
                    g_im = g_im + (p_re * c_im - p_im * c_re)
                r.spread[j, 0, tile + q * CHUNK : tile + (q + 1) * CHUNK] = g_re
                r.spread[j, 1, tile + q * CHUNK : tile + (q + 1) * CHUNK] = g_im
            return carry

        lax.fori_loop(start, stop, one, 0)

    bodies = plan.steps * plan.step_bodies
    turns = bodies // 3
    assert bodies % 3 == 0

    def turn_of(step):
        return max(0, -((4 - step * plan.step_bodies) // 3))

    def turn_after(step):
        return -(-((step + 1) * plan.step_bodies) // 3)

    def pipelined(first, second, third, hooks):
        def most(k):
            third(k, r.mids0)
            second(r.ops1, r.mids1)
            first(k + 2, r.ops2)
            third(k + 1, r.mids1)
            second(r.ops2, r.mids2)

        def turn(i, carry):
            for at, acts in sorted(hooks.items()):
                if at < turns - 1:

                    @pl.when(i == at)
                    def _():
                        for act in acts:
                            act()

            k = 3 * i
            most(k)
            first(k + 3, r.ops0)
            third(k + 2, r.mids2)
            second(r.ops0, r.mids0)
            first(k + 4, r.ops1)
            return carry

        first(0, r.ops0)
        second(r.ops0, r.mids0)
        first(1, r.ops1)
        lax.fori_loop(0, turns - 1, turn, 0)
        for act in hooks.get(turns - 1, ()):
            act()
        most(bodies - 3)
        third(bodies - 1, r.mids2)
        for act in hooks.get(turns, ()):
            act()

    def forward(it, order, hooks):
        def first(k, ops):
            waves(it, k, order, ops)

        def second(ops, mids):
            half_way(r.fwd, ops, mids)

        def third(k, mids):
            spectra(k, order, mids)

        pipelined(first, second, third, hooks)

    def backward(it, hooks):
        def shrinks(i, carry):
            for n in range(2):
                j = 2 * i + n
                r.shrink[j] = 1.0 - r.amp[j] / jnp.sqrt(r.shrink[j] + SOFT_FLOOR)
            return carry

        lax.fori_loop(0, plan.count // 2, shrinks, 0)

        def first(k, ops):
            residuals(k, in_turn, ops)

        def second(ops, mids):
            half_way(r.inv, ops, mids)

        def third(k, mids):
            changes(it, k, in_turn, mids)

        pipelined(first, second, third, hooks)

    def in_turn(t):
        return t

    class Hooks(dict):
        def put(self, at, act, *rest):
            self.setdefault(min(max(at, 0), turns), []).append(functools.partial(act, *rest))

    last = plan.steps - 1

    def each(act, it, step):
        for b in blocks_of(step):
            act(it, b)

    def forward_hooks(it, order):
        hooks = Hooks()
        for t in range(1, plan.steps):
            need = turn_of(t)
            hooks.put(need - 1, each, pass_cores, it, order(t))
            hooks.put(need, each, got_cores, it, order(t))
        for w in range(plan.weights):
            hooks.put(turns // 3, reduce_b, weights, it, w)
            hooks.put(turns - 2, reduce_weights, it, w)
        return hooks

    def backward_hooks(it):
        hooks = Hooks()
        for t in range(plan.steps):
            for b in blocks_of(t):
                hooks.put(turn_after(t), reduce_a, grads, it, b)
                if t < last:
                    hooks.put(turn_after(t + 1), reduce_b, grads, it, b)
        hooks.put(turns // 2, settle_weights, it)
        return hooks

    def late_sums(it):
        object_terms(it, 0, plan.count // 2)
        for b in blocks_of(last):
            reduce_b(grads, it, b)
        for t in range(plan.steps - 3):
            each(to_owner, it, t)
        object_terms(it, plan.count // 2, plan.count)
        if last >= 2:
            each(to_owner, it, last - 2)
        fold_object(it)
        for t in range(max(0, last - 1), plan.steps):
            each(to_owner, it, t)

    send_object(0)
    spread_rows(0, gy)
    spread_chips(0, gy)
    if plan.step_blocks > 1:
        each(pass_chips, 0, first_order(0))
    each(pass_cores, 0, first_order(0))
    from_neighbours(0, r.halo, r.halo_sem)
    widen(0)
    cut_patches(0)
    for t in range(1, plan.steps):
        each(pass_chips, 0, first_order(t))
    for w in range(plan.weights):
        reduce_a(weights, 0, w)
    for copy in loads[1:]:
        copy.wait()
    each(got_cores, 0, first_order(0))
    forward(0, first_order, forward_hooks(0, first_order))
    fold_weights(0)
    loads[0].wait()
    backward(0, backward_hooks(0))
    late_sums(0)
    for t in range(max(0, last - 1)):
        for b in blocks_of(t):
            renew(b)
    r.obj[1] = new_object(0)
    send_object(1)
    for t in range(max(0, last - 1), plan.steps):
        for b in blocks_of(t):
            renew(b)
    for t in range(max(0, last - 1)):
        each(pass_chips, 1, t)
    from_neighbours(1, r.halo, r.halo_sem)
    widen(1)
    cut_patches(1)
    each(pass_cores, 1, 0)
    for t in range(max(0, last - 1), plan.steps):
        each(pass_chips, 1, t)
    for w in range(plan.weights):
        reduce_a(weights, 1, w)
    each(got_cores, 1, 0)
    forward(1, in_turn, forward_hooks(1, in_turn))
    fold_weights(1)
    backward(1, backward_hooks(1))
    late_sums(1)
    final = new_object(1)
    object_out[0] = final[:, :tile]
    object_out[1] = half_turn(final)[:, :tile]
    new = owned(1, gy)
    for plane in range(2):
        if plan.split:
            probe_out[plane] = new[plane]
        else:
            probe_out[plane] = jnp.where(core == 0, new[plane][: plan.own], new[plane][plan.own :])

    for it in range(ITERS):
        sent_to_neighbours(it, r.halo, r.halo_sem)
        sent_to_neighbours(it, r.fold_rx, r.fold_sem)
        sent_to_neighbours(it, r.wfold_rx, r.wfold_sem)
        for ch, blocks in ((grads, plan.gy), (weights, plan.weights)):
            for b in range(blocks):
                await_bytes(ch.rx_a.at[it, b], ch.a_sem.at[0, it, b])
                await_bytes(ch.rx_b.at[it, b], ch.b_sem.at[0, it, b])
        for w in range(plan.weights):
            await_bytes(weights.rx_c.at[it, w], weights.c_sem.at[0, it, w])
        for b in range(plan.gy):

            @pl.when(gy != b)
            def _():
                await_bytes(grads.sum_b.at[it, b], grads.c_sem.at[0, it, b])

            await_bytes(probe_span(it, chips - 1), r.gb_sem.at[0, it, b])
            if plan.split:
                await_bytes(probe_span(it, chips), r.ga_sem.at[0, it, b])
        await_bytes(probe_span(it, ny - 1), r.row_sem.at[it, ny])


def table(side):
    index = np.arange(side, dtype=np.int32)
    angles = (index[:, None] * index[None, :] % side).astype(np.float32) * np.float32(2.0 * math.pi / side)
    factor = np.float32(1.0 / math.sqrt(side))
    cosine, sine = np.cos(angles) * factor, np.sin(angles) * factor
    forward = np.block([[cosine, sine], [-sine, cosine]])
    return jnp.asarray(forward, BF16), jnp.asarray(forward.T, BF16)


def solution(mesh):
    def whole(object_field, probe_modes, positions, amplitudes):
        plan = Plan(mesh, object_field, probe_modes, positions, amplitudes)
        scratch = plan.scratch()

        def local(object_tile, own, places, measured):
            if not plan.split:
                groups = [[2 * i, 2 * i + 1] for i in range(plan.chips)]
                own = lax.all_gather(own, "gx", axis_index_groups=groups, axis=1, tiled=True)
            forward, inverse = table(plan.side)
            vmem = pl.BlockSpec(memory_space=pltpu.VMEM)
            hbm = pl.BlockSpec(memory_space=pl.ANY)
            return pl.pallas_call(
                functools.partial(program, plan, tuple(scratch)),
                out_shape=(
                    jax.ShapeDtypeStruct(object_tile.shape, F32),
                    jax.ShapeDtypeStruct((2, plan.own, plan.side), F32),
                ),
                in_specs=[pl.BlockSpec(memory_space=pltpu.SMEM), vmem, vmem, hbm, hbm, hbm],
                out_specs=(vmem, vmem),
                scratch_shapes=list(scratch.values()),
                compiler_params=pltpu.CompilerParams(
                    collective_id=0, has_side_effects=True, vmem_limit_bytes=56 * 1024 * 1024
                ),
                name="iterations",
            )(
                places.reshape(-1, 2),
                object_tile,
                own,
                measured.reshape(-1, plan.side, plan.side),
                forward,
                inverse,
            )

        return jax.shard_map(
            local,
            mesh=mesh,
            in_specs=(
                P(None, "gy", "gx"),
                P(None, ("gy", "gx"), None),
                P("gy", "gx", None, None),
                P("gy", "gx", None, None, None),
            ),
            out_specs=(P(None, "gy", "gx"), P(None, ("gy", "gx"), None)),
            check_vma=False,
        )(object_field, probe_modes, positions, amplitudes)

    return whole
```

time: 195 us -> 79.9 us (0.41)
  starting transfers between devices: 72.5 us -> 0 us
  waiting for transfers between devices: 63.8 us -> 0 us
  Pallas kernels: 40 us -> 74.7 us
  other arithmetic: 8.1 us -> 0 us
  local copies, waits for them, and re-layouts: 8.44 us -> 3.46 us
    all_to_all x8 -> x0, waiting for transfers between devices: 48.9 us -> none  [the longest x4 18.9 us: whole_of(): blocks = lax.all_to_all(copies, axis, 0, 0, tiled=True)]
    ppermute x16 -> x0, starting transfers between devices: 36.9 us -> none  [the longest x4 16.2 us: extended_2(): before = lax.ppermute(last, axis, up)]
    all_to_all x8 -> x0, starting transfers between devices: 35.7 us -> none  [the longest x4 15.1 us: whole_of(): blocks = lax.all_to_all(copies, axis, 0, 0, tiled=True)]
    pallas_call x2 -> x1, Pallas kernels: 40 us -> 74.7 us  [local(): pl.pallas_call(functools.partial(program, plan, tuple(scratch)), out_shap...]
    ppermute x16 -> x0, waiting for transfers between devices: 15 us -> none  [the longest x8 11.4 us: from_behind(): return lax.ppermute(block, axis, route)]
    broadcast_in_dim x4 -> x0, local copies, waits for them, and re-layouts: 4.29 us -> none  [whole_of(): jnp.broadcast_to(blocks[None], (lax.axis_size(axis), *blocks.shape))]
    transpose x2 -> x0, other arithmetic: 2.71 us -> none  [scattered_sum(): terms = terms.transpose(2, 0, 1, 3, 4)]
    unnamed x14 -> x6, local copies, waits for them, and re-layouts: 0.11 us -> 2.77 us
  transfers between devices with their start and end apart: 24 -> 0, of which waited for: 15 -> 0; matrix products, arithmetic and copies ran while one was open for 6% -> 0% of each run, Pallas kernels for 0% -> 0%
where the time goes in v1:
time: 79.9 us; the launch traced here: 78.8 us
  Pallas kernels  74.7 us (93%)
  local copies, waits for them, and re-layouts  3.46 us (4%)
    pallas_call x1, Pallas kernels, local(): pl.pallas_call(functools.partial(program, plan, tuple(scratch)), out_shap...  74.7 us
    unnamed x6, local copies, waits for them, and re-layouts  2.77 us

profile of v1, /device:TPU:0, one launch (start us, length us, event | category | flops | bytes accessed | tf_op | source)
XLA Modules:
  0.0 78.8 jit_solution(14462259329440024446)
XLA Ops:
  0.6 0.0 copy-start.1
  0.6 0.7 copy-done.1
  1.3 0.7 copy.8.places
  2.0 74.7 %iterations.1 = (f32[2,64,64]{2,1,0:T(8,128)}, f32[2,32,128]{2,1,0:T(8,128)}) custom-call(s32[12,2]{1,0:T(8,128)} %copy.8.places, f32[2,64,64]{2,1,0:T(8,128)} %object_ref.1, f32[2,32,128]{2,1,0:T(8,128)} %own_ref.1, f32[12,128,128]{2,1,0:T(8,128)} %bitcast.2, bf16[256,256]{1,0:T(8,128)(2,1)} %constant.4.clone.fwd_hbm, bf16[256,256]{1,0:T(8,128)(2,1)} %constant.5.clone.inv_hbm), custom_call_target="tpu_custom_call" | custom-call | tf_op jit(solution)/shard_map/iterations/pallas_call | solution.py:902
  76.7 0.0 copy-start
  76.7 1.5 %copy.11 = f32[2,64,64]{2,1,0:T(8,128)} copy(f32[2,64,64]{2,1,0:T(8,128)} %get-tuple-element.4) | data formatting | bytes 65536
  78.2 0.0 copy-done
  78.2 0.6 copy.12
Async XLA Ops:
  0.6 0.7 copy-start.1
  76.7 1.5 %copy-start = (f32[2,32,128]{2,1,0:T(8,128)S(1)}, f32[2,32,128]{2,1,0:T(8,128)}, u32[]{:S(2)}) copy-start(f32[2,32,128]{2,1,0:T(8,128)} %get-tuple-element.5) | copy-start | bytes 98308
